TPU v7x, 512 devices: a whole 4x8x8 slice. The times are simulated.
512 devices in a mesh: ep: 8 (over y_lo, x), tp: 8 (over z), dp: 8 (over y_hi, core).
Axes of the slice: x: 4, y: 8 (y_hi: 4, y_lo: 2; y = y_hi * 2 + y_lo), z: 8, core: 2. Of those that a mesh axis runs over, the one named last changes fastest.
Arguments:
- down_weight: bfloat16 [8, 16384, 3072], P('ep', 'tp', 'dp'), may hold values from -130 to 130
- owned_span: int32 [8, 8, 8], replicated, may hold values from 0 to 511, as said below
Outputs:
- saved_spans: bfloat16 [8, 8, 384, 16384], P('ep', 'tp', 'dp')
Inputs may be any that keep to these rules, and one draw needn't show every extreme that they name: `owned_span`: block g holds rows (g % 64) * 48 onward of expert g // 64; every block is stored by exactly one device; the block at [i, j, k] has (g % 64) // 8 == k; for each k the experts of the stored blocks form a Latin square over i and j: each expert once for each i and once for each j.
All inputs are finite; a program needn't handle non-finite values.
Results may differ from a plain program's by a relative error of at most 0.001.
Values may be sent and summed in bfloat16 or wider, within the bound.
A program may use at most 64 MiB of HBM per device.

v0:
```python
import jax
import jax.numpy as jnp
from jax import lax
from jax.sharding import PartitionSpec as P


def local(down_weight, owned_span):
    local_rows = down_weight[0]
    tp_count = lax.axis_size("tp")
    dp_count = lax.axis_size("dp")
    per_expert = tp_count * dp_count
    hidden_rows = local_rows.shape[0]
    block_rows = local_rows.shape[1] // tp_count
    my_expert = lax.axis_index("ep")
    my_replica = lax.axis_index("dp")
    row_table = lax.dynamic_index_in_dim(owned_span, my_replica, 2, keepdims=False)
    experts_of = row_table // per_expert
    span_of = row_table % per_expert - my_replica * tp_count
    matches = experts_of == my_expert
    wanted = jnp.sum(jnp.where(matches, span_of, 0), axis=1)
    blocks = jnp.transpose(local_rows).reshape(tp_count, block_rows, hidden_rows)
    blocks_out = jnp.take(blocks, wanted, axis=0)
    arrived = lax.all_to_all(blocks_out, "ep", split_axis=0, concat_axis=0, tiled=True)
    expert_order = lax.dynamic_index_in_dim(experts_of, my_expert, 0, keepdims=False)
    regrouped = jnp.take(arrived, expert_order, axis=0)
    columns_in = lax.all_to_all(regrouped, "tp", split_axis=0, concat_axis=0, tiled=True)
    saved_block = jnp.transpose(columns_in, (1, 0, 2)).reshape(block_rows, tp_count * hidden_rows)
    return saved_block[None, None]


def solution(mesh):
    return jax.shard_map(
        local,
        mesh=mesh,
        in_specs=(P("ep", "tp", "dp"), P()),
        out_specs=P("ep", "tp", "dp", None),
        check_vma=False,
    )
```

profile of v0, /device:TPU:16, one launch (start us, length us, event | category | flops | bytes accessed | tf_op | source)
XLA Modules:
  0.0 84.4 jit_solution(15045835260987107419)
XLA Ops:
  0.0 0.0 copy-start
  0.0 0.8 copy-done
  0.8 0.1 constant_dynamic-slice_fusion
  0.8 0.1 copy.9
  1.0 0.1 add_select_fusion.1
  1.1 1.7 %copy.7 = bf16[1,2048,384]{1,2,0:T(8,128)(2,1)S(1)} copy(bf16[1,2048,384]{2,1,0:T(8,128)(2,1)} %param.4) | data formatting | bytes 3145728 | tf_op args[0]
  2.8 0.6 gather_fusion
  3.5 1.4 %broadcast_select_fusion.1 = bf16[8,48,2048]{2,1,0:T(8,128)(2,1)} fusion(bf16[8,48,2048]{2,1,0:T(8,128)(2,1)S(1)} %gather_fusion, pred[8]{0:T(512)(128)(4,1)S(1)} %compare_and_fusion.1), kind=kLoop, calls=%fused_computation.3 | loop fusion | flops 786432 | bytes 3145736 | tf_op jit(solution)/shard_map/jit(_take)/select_n | solution.py:22
  4.9 5.3 %all-to-all-start = ((bf16[8,48,2048]{2,1,0:T(8,128)(2,1)}), bf16[8,48,2048]{2,1,0:T(8,128)(2,1)S(1)}, u32[]{:S(2)}, u32[]{:S(2)}) async-start(bf16[8,48,2048]{2,1,0:T(8,128)(2,1)} %broadcast_select_fusion.1), calls=%async_computation | async-start | bytes 3145728 | tf_op jit(solution)/shard_map/all_to_all | solution.py:23
  10.2 20.4 %all-to-all-done = bf16[8,48,2048]{2,1,0:T(8,128)(2,1)S(1)} async-done(((bf16[8,48,2048]{2,1,0:T(8,128)(2,1)}), bf16[8,48,2048]{2,1,0:T(8,128)(2,1)S(1)}, u32[]{:S(2)}, u32[]{:S(2)}) %all-to-all-start) | async-done | bytes 1572896 | tf_op jit(solution)/shard_map/all_to_all | solution.py:23
  30.6 0.6 gather_fusion.1
  31.2 0.2 broadcast_select_fusion
  31.5 50.0 %all_to_all.10 = bf16[8,48,2048]{2,1,0:T(8,128)(2,1)S(1)} all-to-all(bf16[8,48,2048]{2,1,0:T(8,128)(2,1)S(1)} %broadcast_select_fusion), channel_id=1, replica_groups=mesh['ep'=8,'tp'=8,'dp'=8] {'tp'}, dimensions={0} | all-to-all | bytes 3145728 | tf_op jit(solution)/shard_map/all_to_all | solution.py:26
  81.4 0.9 %copy.8 = bf16[48,8,2048]{2,1,0:T(8,128)(2,1)S(1)} copy(bf16[48,8,2048]{2,0,1:T(8,128)(2,1)S(1)} %bitcast.37) | data formatting | bytes 3145728 | tf_op jit(solution)/shard_map/transpose | solution.py:27
  82.3 2.1 %broadcast_in_dim_reshape.3 = bf16[1,1,48,16384]{3,2,1,0:T(8,128)(2,1)} reshape(bf16[48,8,2048]{2,1,0:T(8,128)(2,1)S(1)} %copy.8) | data formatting | bytes 3145728 | tf_op jit(solution)/shard_map/broadcast_in_dim;reshape | solution.py:28
  (5 shorter events, 0.0 us)
Async XLA Ops:
  0.0 0.8 copy-start
  4.9 25.7 %all-to-all-start = ((bf16[8,48,2048]{2,1,0:T(8,128)(2,1)}), bf16[8,48,2048]{2,1,0:T(8,128)(2,1)S(1)}, u32[]{:S(2)}, u32[]{:S(2)}) async-start(bf16[8,48,2048]{2,1,0:T(8,128)(2,1)} %broadcast_select_fusion.1), calls=%async_computation | async-start | bytes 3145728 | tf_op jit(solution)/shard_map/all_to_all | solution.py:23
where the time goes:
time: 84.7 us; the launch traced here: 84.4 us
  blocking collectives  50 us (59%)
  waiting for transfers between devices  20.4 us (24%)
  local copies, waits for them, and re-layouts  6.92 us (8%)
  starting transfers between devices  5.31 us (6%)
  other arithmetic  1.74 us (2%)
    all_to_all x1, blocking collectives, local(): lax.all_to_all(regrouped, 'tp', split_axis=0, concat_axis=0, tiled=True)  50 us
    all_to_all x1, waiting for transfers between devices, local(): lax.all_to_all(blocks_out, 'ep', split_axis=0, concat_axis=0, tiled=True)  20.4 us
    all_to_all x1, starting transfers between devices, local(): lax.all_to_all(blocks_out, 'ep', split_axis=0, concat_axis=0, tiled=True)  5.31 us
    unnamed x4, local copies, waits for them, and re-layouts  2.59 us
    another operation x1, local copies, waits for them, and re-layouts, local(): return saved_block[None, None]  2.09 us
  transfers between devices with their start and end apart: 1, of which 1 were waited for; matrix products, arithmetic and copies ran while one was open for 0% of the time, Pallas kernels for 0%

commit v1 on v0

v1 whole, which is shorter than its diff:
```python
import functools

import jax
import jax.numpy as jnp
from jax import lax
from jax.experimental import pallas as pl
from jax.experimental.pallas import tpu as pltpu
from jax.sharding import PartitionSpec as P

MESH = pl.DeviceIdType.MESH
HIDDEN = 2048
ROWS = 384
SPANS = 8
BLOCK = 48
CHUNKS = (128, 128, 256, 512, 512, 512)
STARTS = tuple(sum(CHUNKS[:n]) for n in range(len(CHUNKS)))
EP_STEPS = ((1, 2), (1, 1), (1, 3), (0, 2), (1, 0), (0, 1), (0, 3))
TP_STEPS = (1, 7, 2, 6, 3, 5, 4)


def ep_member(index, step):
    half, along = lax.div(index, 4), lax.rem(index, 4)
    return lax.rem(half + step[0], 2) * 4 + lax.rem(along + step[1], 4)


def kernel(weight, span, out, x_in, table, turned, *rest):
    count = len(CHUNKS)
    send_one, recv_one, send_two = rest[:count], rest[count : 2 * count], rest[2 * count : 3 * count]
    in_sem, table_sem, ss_one, rs_one, ss_two, rs_two = rest[3 * count :]
    my_ep = lax.axis_index("ep")
    my_tp = lax.axis_index("tp")
    my_dp = lax.axis_index("dp")

    barrier = pltpu.get_barrier_semaphore()
    for step in EP_STEPS:
        pl.semaphore_signal(barrier, inc=1, device_id={"ep": ep_member(my_ep, step)}, device_id_type=MESH)
    for step in TP_STEPS:
        pl.semaphore_signal(barrier, inc=1, device_id={"tp": lax.rem(my_tp + step, 8)}, device_id_type=MESH)

    table_copy = pltpu.make_async_copy(span, table, table_sem)
    table_copy.start()
    loads = []
    for c, (start, width) in enumerate(zip(STARTS, CHUNKS)):
        load = pltpu.make_async_copy(weight.at[0, pl.ds(start, width)], x_in.at[pl.ds(start, width)], in_sem.at[c])
        load.start()
        loads.append(load)
    table_copy.wait()

    def span_for(member):
        found = 0
        for j in range(8):
            owned = table[member, j, my_dp]
            mine = 1 - lax.min(lax.abs(lax.div(owned, 64) - my_ep), 1)
            found += mine * lax.rem(owned, SPANS)
        return found

    members = [my_ep] + [ep_member(my_ep, step) for step in EP_STEPS]
    spans = [span_for(member) for member in members]
    targets = [my_tp] + [lax.rem(my_tp + step, 8) for step in TP_STEPS]
    experts = [lax.div(table[my_ep, target, my_dp], 64) for target in targets]

    sends_one, sends_two = [], []
    for c, (start, width) in enumerate(zip(STARTS, CHUNKS)):
        loads[c].wait()
        turned[:, :, pl.ds(start, width)] = jnp.transpose(x_in[pl.ds(start, width), :]).reshape(SPANS, BLOCK, width)
        for n, member in enumerate(members):
            block = turned[spans[n], :, pl.ds(start, width)]
            if n == 0:
                recv_one[c][my_ep] = block
            else:
                send_one[c][n - 1] = block
        if c == 0:
            pl.semaphore_wait(barrier, 14)
        for n, member in enumerate(members[1:]):
            copy = pltpu.make_async_remote_copy(
                src_ref=send_one[c].at[n],
                dst_ref=recv_one[c].at[my_ep],
                send_sem=ss_one.at[c, n],
                recv_sem=rs_one.at[c, n],
                device_id={"ep": member},
                device_id_type=MESH,
            )
            copy.start()
            sends_one.append(copy)

    for c, (start, width) in enumerate(zip(STARTS, CHUNKS)):
        for n in range(7):
            sends_one[c * 7 + n].wait_recv()
        for n, target in enumerate(targets):
            block = recv_one[c][experts[n]]
            if n == 0:
                mine = pl.multiple_of(my_tp * HIDDEN + start, 128)
                out[:, pl.ds(mine, width)] = block
            else:
                send_two[c][n - 1] = block
        for n, target in enumerate(targets[1:]):
            copy = pltpu.make_async_remote_copy(
                src_ref=send_two[c].at[n],
                dst_ref=out.at[:, pl.ds(pl.multiple_of(my_tp * HIDDEN + start, 128), width)],
                send_sem=ss_two.at[c, n],
                recv_sem=rs_two.at[c, n],
                device_id={"tp": target},
                device_id_type=MESH,
            )
            copy.start()
            sends_two.append(copy)

    for copy in sends_one:
        copy.wait_send()
    for copy in sends_two:
        copy.wait()


def local(down_weight, owned_span):
    count = len(CHUNKS)
    slots = lambda number: [pltpu.VMEM((number, BLOCK, width), jnp.bfloat16) for width in CHUNKS]
    saved = pl.pallas_call(
        kernel,
        out_shape=pltpu.VMEM((BLOCK, 8 * HIDDEN), jnp.bfloat16),
        in_specs=[pl.BlockSpec(memory_space=pltpu.HBM), pl.BlockSpec(memory_space=pltpu.HBM)],
        out_specs=pl.BlockSpec(memory_space=pltpu.VMEM),
        scratch_shapes=[
            pltpu.VMEM((HIDDEN, ROWS), jnp.bfloat16),
            pltpu.SMEM((8, 8, 8), jnp.int32),
            pltpu.VMEM((SPANS, BLOCK, HIDDEN), jnp.bfloat16),
            *slots(7),
            *slots(8),
            *slots(7),
            pltpu.SemaphoreType.DMA((count,)),
            pltpu.SemaphoreType.DMA,
            pltpu.SemaphoreType.DMA((count, 7)),
            pltpu.SemaphoreType.DMA((count, 7)),
            pltpu.SemaphoreType.DMA((count, 7)),
            pltpu.SemaphoreType.DMA((count, 7)),
        ],
        compiler_params=pltpu.CompilerParams(collective_id=0, has_side_effects=True, vmem_limit_bytes=60 << 20),
    )(down_weight, owned_span)
    return saved[None, None]


def solution(mesh):
    return jax.shard_map(
        local,
        mesh=mesh,
        in_specs=(P("ep", "tp", "dp"), P()),
        out_specs=P("ep", "tp", "dp", None),
        check_vma=False,
    )
```

time: 84.7 us -> 54.6 us (0.64)
  the two profiles are of different devices: /device:TPU:16 before, /device:TPU:48 now
where the time goes in v1:
time: 54.6 us; the launch traced here: 54.5 us
  Pallas kernels  53.3 us (98%)
  local copies, waits for them, and re-layouts  1.15 us (2%)
    pallas_call x1, Pallas kernels, local(): pl.pallas_call(kernel, out_shape=pltpu.VMEM((BLOCK, 8 * HIDDEN), jnp.bflo...  53.3 us
    unnamed x1, local copies, waits for them, and re-layouts  1.15 us

profile of v1, /device:TPU:48, one launch (start us, length us, event | category | flops | bytes accessed | tf_op | source)
XLA Modules:
  0.0 54.5 jit_solution(1857813843474773268)
XLA Ops:
  0.0 53.3 %shard_map.28 = bf16[48,16384]{1,0:T(8,128)(2,1)S(1)} custom-call(bf16[1,2048,384]{2,1,0:T(8,128)(2,1)} %weight.1, s32[8,8,8]{2,1,0:T(8,128)} %span.1), custom_call_target="tpu_custom_call" | custom-call | tf_op jit(solution)/shard_map/pallas_call | solution.py:117
  53.3 1.1 %copy.4 = bf16[1,1,48,16384]{3,2,1,0:T(8,128)(2,1)} copy(bf16[1,1,48,16384]{3,2,1,0:T(8,128)(2,1)S(1)} %bitcast.1) | data formatting | bytes 3145728

commit v2 on v0

v2 whole, which is shorter than its diff:
```python
import jax
import jax.numpy as jnp
from jax import lax
from jax.experimental import pallas as pl
from jax.experimental.pallas import tpu as pltpu
from jax.sharding import PartitionSpec as P

LOGICAL = pl.DeviceIdType.LOGICAL
HIDDEN = 2048
ROWS = 384
SPANS = 8
BLOCK = 48
FIRST = 384
CHUNKS = (256, 384, 512, 512)
EARLY = 1
ORDERS = ("asc",) * 5
SCATTER = 1
STARTS = tuple(FIRST + sum(CHUNKS[:n]) for n in range(len(CHUNKS)))
EP_STEPS = ((1, 2), (1, 1), (1, 3), (0, 2), (1, 0), (0, 1), (0, 3))
TP_STEPS = (1, 7, 2, 6, 3, 5, 4)


def ep_member(index, step):
    return ((index + 4 * step[0]) & 4) + ((index + step[1]) & 3)


def others(index):
    return [n + ((n - index + 8) >> 3) for n in range(7)]


def kernel(weight, span, out, x_in, table, turned, z_send, z_recv, z_mid, z_last, *rest):
    count = len(CHUNKS)
    send_one, recv_one, send_two = rest[:count], rest[count : 2 * count], rest[2 * count : 3 * count]
    in_sem, table_sem, ss_one, rs_one, ss_two, rs_two, ss_z, rs_z = rest[3 * count :]
    my_ep = lax.axis_index("ep")
    my_tp = lax.axis_index("tp")
    my_dp = lax.axis_index("dp")

    members = [ep_member(my_ep, step) for step in EP_STEPS]
    ep_ids = [member * 64 + my_tp * 8 + my_dp for member in members]
    tp_orders = {"near": [(my_tp + step) & 7 for step in TP_STEPS], "asc": others(my_tp)}
    sources = tp_orders["near"]

    def tp_id(target):
        return my_ep * 64 + target * 8 + my_dp

    barrier = pltpu.get_barrier_semaphore()
    for other in [tp_id(target) for target in tp_orders["near"][::-1]] + ep_ids:
        pl.semaphore_signal(barrier, inc=1, device_id=other, device_id_type=LOGICAL)

    table_copy = pltpu.make_async_copy(span, table, table_sem)
    table_copy.start()
    parts = [(0, FIRST)] + list(zip(STARTS, CHUNKS))
    loads = []
    for c, (start, width) in enumerate(parts):
        load = pltpu.make_async_copy(weight.at[0, pl.ds(start, width)], x_in.at[pl.ds(start, width)], in_sem.at[c])
        load.start()
        loads.append(load)
    table_copy.wait()

    def expert_of(member, target):
        return table[member, target, my_dp] >> 6

    def span_if_mine(member, target):
        owned = table[member, target, my_dp]
        return (1 - lax.min(lax.abs((owned >> 6) - my_ep), 1)) * (owned & 7)

    def span_for_member(member):
        return sum(span_if_mine(member, j) for j in range(8))

    def span_for_target(target):
        return sum(span_if_mine(i, target) for i in range(8))

    def turn(part):
        start, width = parts[part]
        loads[part].wait()
        turned[:, :, pl.ds(start, width)] = jnp.transpose(x_in[pl.ds(start, width), :]).reshape(SPANS, BLOCK, width)

    def remote(src, dst, send_sem, recv_sem, other):
        return pltpu.make_async_remote_copy(
            src_ref=src, dst_ref=dst, send_sem=send_sem, recv_sem=recv_sem, device_id=other, device_id_type=LOGICAL
        )

    started, awaited = [], []

    turn(0)
    z_targets = tp_orders[ORDERS[0]]
    z_recv[my_tp] = turned[span_for_target(my_tp), :, pl.ds(0, FIRST)]
    for n, target in enumerate(z_targets):
        z_send[n] = turned[span_for_target(target), :, pl.ds(0, FIRST)]

    spans = [span_for_member(member) for member in [my_ep] + members]

    def stage(c):
        turn(c + 1)
        start, width = STARTS[c], CHUNKS[c]
        recv_one[c][my_ep] = turned[spans[0], :, pl.ds(start, width)]
        for n in range(7):
            send_one[c][n] = turned[spans[n + 1], :, pl.ds(start, width)]

    for c in range(EARLY):
        stage(c)
    pl.semaphore_wait(barrier, 14)

    for n, target in enumerate(z_targets):
        copy = remote(z_send.at[n], z_recv.at[my_tp], ss_z.at[0, n], rs_z.at[0, my_tp], tp_id(target))
        copy.start()
        started.append(copy)

    one = []
    for c in range(count):
        if c >= EARLY:
            stage(c)
        for n, other in enumerate(ep_ids):
            copy = remote(send_one[c].at[n], recv_one[c].at[my_ep], ss_one.at[c, n], rs_one.at[c, n], other)
            copy.start()
            started.append(copy)
            one.append(copy)

    def columns(shard, start, width):
        return pl.ds(pl.multiple_of(shard * HIDDEN + start, 128), width)

    for c in range(count):
        start, width = STARTS[c], CHUNKS[c]
        for n in range(7):
            one[c * 7 + n].wait_recv()
        targets = tp_orders[ORDERS[c + 1]]
        for n, target in enumerate(targets):
            send_two[c][n] = recv_one[c][expert_of(my_ep, target)]
        for n, target in enumerate(targets):
            mine = out.at[:, columns(my_tp, start, width)]
            copy = remote(send_two[c].at[n], mine, ss_two.at[c, n], rs_two.at[c, my_tp], tp_id(target))
            copy.start()
            started.append(copy)
        out[:, columns(my_tp, start, width)] = recv_one[c][expert_of(my_ep, my_tp)]
        for source in sources:
            theirs = out.at[:, columns(source, start, width)]
            awaited.append(remote(send_two[c].at[0], theirs, ss_two.at[c, 0], rs_two.at[c, source], tp_id(source)))

        if c == SCATTER:
            for source in sources:
                remote(z_send.at[0], z_recv.at[source], ss_z.at[0, 0], rs_z.at[0, source], tp_id(source)).wait_recv()
            for n, member in enumerate(members):
                copy = remote(z_recv.at[member], z_mid.at[my_ep], ss_z.at[1, n], rs_z.at[1, n], ep_ids[n])
                copy.start()
                started.append(copy)
            z_mid[my_ep] = z_recv[my_ep]

    for n, member in enumerate(members):
        remote(z_recv.at[0], z_mid.at[member], ss_z.at[1, n], rs_z.at[1, n], ep_ids[n]).wait_recv()
    for n, member in enumerate(members):
        z_last[n] = z_mid[expert_of(member, my_tp)]
    for n, member in enumerate(members):
        mine = out.at[:, columns(my_ep, 0, FIRST)]
        copy = remote(z_last.at[n], mine, ss_z.at[2, n], rs_z.at[2, n], ep_ids[n])
        copy.start()
        started.append(copy)
    out[:, columns(my_ep, 0, FIRST)] = z_mid[expert_of(my_ep, my_tp)]
    for n, member in enumerate(members):
        theirs = out.at[:, columns(member, 0, FIRST)]
        awaited.append(remote(z_last.at[n], theirs, ss_z.at[2, n], rs_z.at[2, n], ep_ids[n]))

    for copy in awaited:
        copy.wait_recv()
    for copy in started:
        copy.wait_send()


def local(down_weight, owned_span):
    count = len(CHUNKS)

    def slots(number, width):
        return pltpu.VMEM((number, BLOCK, width), jnp.bfloat16)

    saved = pl.pallas_call(
        kernel,
        out_shape=pltpu.VMEM((BLOCK, 8 * HIDDEN), jnp.bfloat16),
        in_specs=[pl.BlockSpec(memory_space=pltpu.HBM), pl.BlockSpec(memory_space=pltpu.HBM)],
        out_specs=pl.BlockSpec(memory_space=pltpu.VMEM),
        scratch_shapes=[
            pltpu.VMEM((HIDDEN, ROWS), jnp.bfloat16),
            pltpu.SMEM((8, 8, 8), jnp.int32),
            pltpu.VMEM((SPANS, BLOCK, HIDDEN), jnp.bfloat16),
            slots(7, FIRST),
            slots(8, FIRST),
            slots(8, FIRST),
            slots(7, FIRST),
            *[slots(7, width) for width in CHUNKS],
            *[slots(8, width) for width in CHUNKS],
            *[slots(7, width) for width in CHUNKS],
            pltpu.SemaphoreType.DMA((count + 1,)),
            pltpu.SemaphoreType.DMA,
            pltpu.SemaphoreType.DMA((count, 7)),
            pltpu.SemaphoreType.DMA((count, 7)),
            pltpu.SemaphoreType.DMA((count, 7)),
            pltpu.SemaphoreType.DMA((count, 8)),
            pltpu.SemaphoreType.DMA((3, 7)),
            pltpu.SemaphoreType.DMA((3, 8)),
        ],
        compiler_params=pltpu.CompilerParams(collective_id=0, has_side_effects=True, vmem_limit_bytes=60 << 20),
    )(down_weight, owned_span)
    return saved[None, None]


def solution(mesh):
    return jax.shard_map(
        local,
        mesh=mesh,
        in_specs=(P("ep", "tp", "dp"), P()),
        out_specs=P("ep", "tp", "dp", None),
        check_vma=False,
    )
```

time: 84.7 us -> 49.3 us (0.58)
  the two profiles are of different devices: /device:TPU:16 before, /device:TPU:144 now
where the time goes in v2:
time: 49.3 us; the launch traced here: 48.9 us
  Pallas kernels  47.7 us (97%)
  local copies, waits for them, and re-layouts  1.15 us (2%)
    pallas_call x1, Pallas kernels, local(): pl.pallas_call(kernel, out_shape=pltpu.VMEM((BLOCK, 8 * HIDDEN), jnp.bflo...  47.7 us
    unnamed x1, local copies, waits for them, and re-layouts  1.15 us

profile of v2, /device:TPU:144, one launch (start us, length us, event | category | flops | bytes accessed | tf_op | source)
XLA Modules:
  0.0 48.9 jit_solution(13506789270317605479)
XLA Ops:
  0.0 47.7 %shard_map.28 = bf16[48,16384]{1,0:T(8,128)(2,1)S(1)} custom-call(bf16[1,2048,384]{2,1,0:T(8,128)(2,1)} %weight.1, s32[8,8,8]{2,1,0:T(8,128)} %span.1), custom_call_target="tpu_custom_call" | custom-call | tf_op jit(solution)/shard_map/pallas_call | solution.py:175
  47.8 1.1 %copy.4 = bf16[1,1,48,16384]{3,2,1,0:T(8,128)(2,1)} copy(bf16[1,1,48,16384]{3,2,1,0:T(8,128)(2,1)S(1)} %bitcast.1) | data formatting | bytes 3145728

commit v3 on v2

--- a/solution.py
+++ b/solution.py
@@ -10,11 +10,12 @@
 ROWS = 384
 SPANS = 8
 BLOCK = 48
-FIRST = 384
-CHUNKS = (256, 384, 512, 512)
+FIRST = 640
+CHUNKS = (512, 896)
 EARLY = 1
-ORDERS = ("asc",) * 5
-SCATTER = 1
+LOW = (0, 1, 2, 3, 4, 5, 6, 7)
+ORDERS = (None,) * len(CHUNKS) + (LOW,)
+SCATTER = 0
 STARTS = tuple(FIRST + sum(CHUNKS[:n]) for n in range(len(CHUNKS)))
 EP_STEPS = ((1, 2), (1, 1), (1, 3), (0, 2), (1, 0), (0, 1), (0, 3))
 TP_STEPS = (1, 7, 2, 6, 3, 5, 4)
@@ -24,8 +25,9 @@
     return ((index + 4 * step[0]) & 4) + ((index + step[1]) & 3)
 
 
-def others(index):
-    return [n + ((n - index + 8) >> 3) for n in range(7)]
+def others(index, order):
+    place = sum(n * (1 - lax.min(lax.abs(index - target), 1)) for n, target in enumerate(order))
+    return [order[n] + ((n - place + 8) >> 3) * (order[n + 1] - order[n]) for n in range(7)]
 
 
 def kernel(weight, span, out, x_in, table, turned, z_send, z_recv, z_mid, z_last, *rest):
@@ -38,14 +40,14 @@
 
     members = [ep_member(my_ep, step) for step in EP_STEPS]
     ep_ids = [member * 64 + my_tp * 8 + my_dp for member in members]
-    tp_orders = {"near": [(my_tp + step) & 7 for step in TP_STEPS], "asc": others(my_tp)}
-    sources = tp_orders["near"]
+    sources = [(my_tp + step) & 7 for step in TP_STEPS]
+    tp_orders = [sources if order is None else others(my_tp, order) for order in ORDERS]
 
     def tp_id(target):
         return my_ep * 64 + target * 8 + my_dp
 
     barrier = pltpu.get_barrier_semaphore()
-    for other in [tp_id(target) for target in tp_orders["near"][::-1]] + ep_ids:
+    for other in [tp_id(target) for target in sources[::-1]] + ep_ids:
         pl.semaphore_signal(barrier, inc=1, device_id=other, device_id_type=LOGICAL)
 
     table_copy = pltpu.make_async_copy(span, table, table_sem)
@@ -84,7 +86,7 @@
     started, awaited = [], []
 
     turn(0)
-    z_targets = tp_orders[ORDERS[0]]
+    z_targets = tp_orders[0]
     z_recv[my_tp] = turned[span_for_target(my_tp), :, pl.ds(0, FIRST)]
     for n, target in enumerate(z_targets):
         z_send[n] = turned[span_for_target(target), :, pl.ds(0, FIRST)]
@@ -124,7 +126,7 @@
         start, width = STARTS[c], CHUNKS[c]
         for n in range(7):
             one[c * 7 + n].wait_recv()
-        targets = tp_orders[ORDERS[c + 1]]
+        targets = tp_orders[c + 1]
         for n, target in enumerate(targets):
             send_two[c][n] = recv_one[c][expert_of(my_ep, target)]
         for n, target in enumerate(targets):

time: 49.3 us -> 48.5 us (0.984)
  Pallas kernels: 47.7 us -> 47.2 us
    pallas_call x1, Pallas kernels: 47.7 us -> 47.2 us  [local(): pl.pallas_call(kernel, out_shape=pltpu.VMEM((BLOCK, 8 * HIDDEN), jnp.bflo...]
where the time goes in v3:
time: 48.5 us; the launch traced here: 48.4 us
  Pallas kernels  47.2 us (97%)
  local copies, waits for them, and re-layouts  1.15 us (2%)
    pallas_call x1, Pallas kernels, local(): pl.pallas_call(kernel, out_shape=pltpu.VMEM((BLOCK, 8 * HIDDEN), jnp.bflo...  47.2 us
    unnamed x1, local copies, waits for them, and re-layouts  1.15 us

profile of v3, /device:TPU:144, one launch (start us, length us, event | category | flops | bytes accessed | tf_op | source)
XLA Modules:
  0.0 48.4 jit_solution(8030583559351380285)
XLA Ops:
  0.0 47.2 %shard_map.28 = bf16[48,16384]{1,0:T(8,128)(2,1)S(1)} custom-call(bf16[1,2048,384]{2,1,0:T(8,128)(2,1)} %weight.1, s32[8,8,8]{2,1,0:T(8,128)} %span.1), custom_call_target="tpu_custom_call" | custom-call | tf_op jit(solution)/shard_map/pallas_call | solution.py:177
  47.2 1.1 %copy.4 = bf16[1,1,48,16384]{3,2,1,0:T(8,128)(2,1)} copy(bf16[1,1,48,16384]{3,2,1,0:T(8,128)(2,1)S(1)} %bitcast.1) | data formatting | bytes 3145728

commit v4 on v3

--- a/solution.py
+++ b/solution.py
@@ -38,14 +38,12 @@
     my_tp = lax.axis_index("tp")
     my_dp = lax.axis_index("dp")
 
-    members = [ep_member(my_ep, step) for step in EP_STEPS]
-    ep_ids = [member * 64 + my_tp * 8 + my_dp for member in members]
-    sources = [(my_tp + step) & 7 for step in TP_STEPS]
-    tp_orders = [sources if order is None else others(my_tp, order) for order in ORDERS]
-
     def tp_id(target):
         return my_ep * 64 + target * 8 + my_dp
 
+    sources = [(my_tp + step) & 7 for step in TP_STEPS]
+    members = [ep_member(my_ep, step) for step in EP_STEPS]
+    ep_ids = [member * 64 + my_tp * 8 + my_dp for member in members]
     barrier = pltpu.get_barrier_semaphore()
     for other in [tp_id(target) for target in sources[::-1]] + ep_ids:
         pl.semaphore_signal(barrier, inc=1, device_id=other, device_id_type=LOGICAL)
@@ -58,7 +56,8 @@
         load = pltpu.make_async_copy(weight.at[0, pl.ds(start, width)], x_in.at[pl.ds(start, width)], in_sem.at[c])
         load.start()
         loads.append(load)
-    table_copy.wait()
+
+    tp_orders = [sources if order is None else others(my_tp, order) for order in ORDERS]
 
     def expert_of(member, target):
         return table[member, target, my_dp] >> 6
@@ -83,9 +82,11 @@
             src_ref=src, dst_ref=dst, send_sem=send_sem, recv_sem=recv_sem, device_id=other, device_id_type=LOGICAL
         )
 
-    started, awaited = [], []
+    def group_wait(sem, ref):
+        pltpu.make_async_copy(ref, ref, sem).wait()
 
     turn(0)
+    table_copy.wait()
     z_targets = tp_orders[0]
     z_recv[my_tp] = turned[span_for_target(my_tp), :, pl.ds(0, FIRST)]
     for n, target in enumerate(z_targets):
@@ -105,67 +106,51 @@
     pl.semaphore_wait(barrier, 14)
 
     for n, target in enumerate(z_targets):
-        copy = remote(z_send.at[n], z_recv.at[my_tp], ss_z.at[0, n], rs_z.at[0, my_tp], tp_id(target))
-        copy.start()
-        started.append(copy)
+        remote(z_send.at[n], z_recv.at[my_tp], ss_z.at[0], rs_z.at[0], tp_id(target)).start()
 
-    one = []
     for c in range(count):
         if c >= EARLY:
             stage(c)
         for n, other in enumerate(ep_ids):
-            copy = remote(send_one[c].at[n], recv_one[c].at[my_ep], ss_one.at[c, n], rs_one.at[c, n], other)
-            copy.start()
-            started.append(copy)
-            one.append(copy)
+            remote(send_one[c].at[n], recv_one[c].at[my_ep], ss_one.at[c], rs_one.at[c], other).start()
 
     def columns(shard, start, width):
         return pl.ds(pl.multiple_of(shard * HIDDEN + start, 128), width)
 
     for c in range(count):
         start, width = STARTS[c], CHUNKS[c]
-        for n in range(7):
-            one[c * 7 + n].wait_recv()
+        group_wait(rs_one.at[c], recv_one[c].at[pl.ds(0, 7)])
         targets = tp_orders[c + 1]
         for n, target in enumerate(targets):
             send_two[c][n] = recv_one[c][expert_of(my_ep, target)]
         for n, target in enumerate(targets):
             mine = out.at[:, columns(my_tp, start, width)]
-            copy = remote(send_two[c].at[n], mine, ss_two.at[c, n], rs_two.at[c, my_tp], tp_id(target))
-            copy.start()
-            started.append(copy)
+            remote(send_two[c].at[n], mine, ss_two.at[c], rs_two.at[c], tp_id(target)).start()
         out[:, columns(my_tp, start, width)] = recv_one[c][expert_of(my_ep, my_tp)]
-        for source in sources:
-            theirs = out.at[:, columns(source, start, width)]
-            awaited.append(remote(send_two[c].at[0], theirs, ss_two.at[c, 0], rs_two.at[c, source], tp_id(source)))
 
         if c == SCATTER:
-            for source in sources:
-                remote(z_send.at[0], z_recv.at[source], ss_z.at[0, 0], rs_z.at[0, source], tp_id(source)).wait_recv()
+            group_wait(rs_z.at[0], z_recv.at[pl.ds(0, 7)])
             for n, member in enumerate(members):
-                copy = remote(z_recv.at[member], z_mid.at[my_ep], ss_z.at[1, n], rs_z.at[1, n], ep_ids[n])
-                copy.start()
-                started.append(copy)
+                remote(z_recv.at[member], z_mid.at[my_ep], ss_z.at[1], rs_z.at[1], ep_ids[n]).start()
             z_mid[my_ep] = z_recv[my_ep]
 
-    for n, member in enumerate(members):
-        remote(z_recv.at[0], z_mid.at[member], ss_z.at[1, n], rs_z.at[1, n], ep_ids[n]).wait_recv()
+    group_wait(rs_z.at[1], z_mid.at[pl.ds(0, 7)])
     for n, member in enumerate(members):
         z_last[n] = z_mid[expert_of(member, my_tp)]
     for n, member in enumerate(members):
         mine = out.at[:, columns(my_ep, 0, FIRST)]
-        copy = remote(z_last.at[n], mine, ss_z.at[2, n], rs_z.at[2, n], ep_ids[n])
-        copy.start()
-        started.append(copy)
+        remote(z_last.at[n], mine, ss_z.at[2], rs_z.at[2], ep_ids[n]).start()
     out[:, columns(my_ep, 0, FIRST)] = z_mid[expert_of(my_ep, my_tp)]
-    for n, member in enumerate(members):
-        theirs = out.at[:, columns(member, 0, FIRST)]
-        awaited.append(remote(z_last.at[n], theirs, ss_z.at[2, n], rs_z.at[2, n], ep_ids[n]))
 
-    for copy in awaited:
-        copy.wait_recv()
-    for copy in started:
-        copy.wait_send()
+    group_wait(ss_z.at[0], z_send)
+    group_wait(ss_z.at[1], z_recv.at[pl.ds(0, 7)])
+    for c in range(count):
+        group_wait(ss_one.at[c], send_one[c])
+    group_wait(ss_z.at[2], z_last)
+    group_wait(rs_z.at[2], out.at[:, pl.ds(0, 7 * FIRST)])
+    for c, width in enumerate(CHUNKS):
+        group_wait(ss_two.at[c], send_two[c])
+        group_wait(rs_two.at[c], out.at[:, pl.ds(0, 7 * width)])
 
 
 def local(down_weight, owned_span):
@@ -192,12 +177,12 @@
             *[slots(7, width) for width in CHUNKS],
             pltpu.SemaphoreType.DMA((count + 1,)),
             pltpu.SemaphoreType.DMA,
-            pltpu.SemaphoreType.DMA((count, 7)),
-            pltpu.SemaphoreType.DMA((count, 7)),
-            pltpu.SemaphoreType.DMA((count, 7)),
-            pltpu.SemaphoreType.DMA((count, 8)),
-            pltpu.SemaphoreType.DMA((3, 7)),
-            pltpu.SemaphoreType.DMA((3, 8)),
+            pltpu.SemaphoreType.DMA((count,)),
+            pltpu.SemaphoreType.DMA((count,)),
+            pltpu.SemaphoreType.DMA((count,)),
+            pltpu.SemaphoreType.DMA((count,)),
+            pltpu.SemaphoreType.DMA((3,)),
+            pltpu.SemaphoreType.DMA((3,)),
         ],
         compiler_params=pltpu.CompilerParams(collective_id=0, has_side_effects=True, vmem_limit_bytes=60 << 20),
     )(down_weight, owned_span)

time: 48.5 us -> 47.6 us (0.981)
  Pallas kernels: 47.2 us -> 46.3 us
    pallas_call x1, Pallas kernels: 47.2 us -> 46.3 us  [local(): pl.pallas_call(kernel, out_shape=pltpu.VMEM((BLOCK, 8 * HIDDEN), jnp.bflo...]
where the time goes in v4:
time: 47.6 us; the launch traced here: 47.5 us
  Pallas kernels  46.3 us (97%)
  local copies, waits for them, and re-layouts  1.15 us (2%)
    pallas_call x1, Pallas kernels, local(): pl.pallas_call(kernel, out_shape=pltpu.VMEM((BLOCK, 8 * HIDDEN), jnp.bflo...  46.3 us
    unnamed x1, local copies, waits for them, and re-layouts  1.15 us

profile of v4, /device:TPU:144, one launch (start us, length us, event | category | flops | bytes accessed | tf_op | source)
XLA Modules:
  0.0 47.5 jit_solution(669668473805986821)
XLA Ops:
  0.0 46.3 %shard_map.28 = bf16[48,16384]{1,0:T(8,128)(2,1)S(1)} custom-call(bf16[1,2048,384]{2,1,0:T(8,128)(2,1)} %weight.1, s32[8,8,8]{2,1,0:T(8,128)} %span.1), custom_call_target="tpu_custom_call" | custom-call | tf_op jit(solution)/shard_map/pallas_call | solution.py:162
  46.3 1.1 %copy.4 = bf16[1,1,48,16384]{3,2,1,0:T(8,128)(2,1)} copy(bf16[1,1,48,16384]{3,2,1,0:T(8,128)(2,1)S(1)} %bitcast.1) | data formatting | bytes 3145728
